TPU v7x, 32 devices: a whole 2x2x4 slice. The times are simulated.
32 devices in a mesh: section: 4 (over y, core), dp: 8 (over z, x).
Axes of the slice: x: 2, y: 2, z: 4, core: 2. Of those that a mesh axis runs over, the one named last changes fastest.
Arguments:
- student_states: bfloat16 [4, 1024, 2048], P('section', 'dp'), may hold values from -6 to 6
- teacher_states: bfloat16 [16, 1024, 7168], P('section', 'dp'), may hold values from -18 to 18
- projector: bfloat16 [4, 2048, 7168], P('section', None, 'dp'), may hold values from -0.125 to 0.125
- layer_map: int32 [4], replicated, may hold values from 0 to 12, as said below
- boundaries: int32 [5], replicated, may hold values from 0 to 13, as said below
- valid_counts: int32 [8], P('dp'), may hold values from 32 to 128, as said below
Outputs:
- student_grads: bfloat16 [4, 1024, 2048], P('section', 'dp')
- projector_grads: bfloat16 [4, 2048, 7168], P('section', None, 'dp')
- layer_losses: float32 [4], P('section')
Inputs may be any that keep to these rules, and one draw needn't show every extreme that they name: Section k holds 4 or 3 teacher layers, three sections the smaller number; boundaries[0] is 0 and boundaries[4] is 13. Teacher layer layer_map[l] lies on a section from l - 2 to l + 2; student layers 0 and 3 pair with layers of sections 1 and 2, student layers 1 and 2 with layers of sections 3 and 0. `valid_counts`: the valid tokens stand first in their micro-batch; the last micro-batch is full.
All inputs are finite; a program needn't handle non-finite values.
Results may differ from a plain program's by a relative error of at most 0.015.
Values may be sent and summed in bfloat16 or wider, within the bound.
A program may use at most 128 MiB of HBM per device.

v0:
```python
import functools

import jax
import jax.numpy as jnp
from jax import lax
from jax.experimental import pallas as pl
from jax.experimental.pallas import tpu as pltpu
from jax.sharding import PartitionSpec as P

loss_scale = 128.0
norm_eps = 1e-06
MESH = pl.DeviceIdType.MESH
F32, BF16 = jnp.float32, jnp.bfloat16
CHUNKS = 2
GRAD_TILES = 8


def from_behind(block, axis, distance):
    devices = range(lax.axis_size(axis))
    route = [(i - distance, i) for i in devices if i - distance in devices]
    return lax.ppermute(block, axis, route)


def lookup(table, index):
    places = jnp.arange(table.shape[0], dtype=jnp.int32)
    return jnp.sum(jnp.where(places == index, table, 0))


def relayed(teacher_states, layer_map, boundaries):
    sections = lax.axis_size("section")
    here = lax.axis_index("section")
    held_slots = teacher_states.shape[0]
    inner = boundaries[1:sections]
    owners = jnp.sum((inner[None, :] <= layer_map[:, None]).astype(jnp.int32), axis=1)
    first_layer = lookup(boundaries, here)

    def outgoing(offset):
        destination = here + offset
        inside = (destination >= 0) & (destination < sections)
        wanted = lookup(layer_map, destination)
        owner = lookup(owners, destination)
        place = jnp.clip(wanted - first_layer, 0, held_slots - 1)
        piece = lax.dynamic_index_in_dim(teacher_states, place, 0, keepdims=False)
        return jnp.where(inside & (owner == here), piece, jnp.zeros_like(piece))

    needed = here - lookup(owners, here)
    arrivals = []
    for offset in (-1, 1):
        stacked = jnp.stack([outgoing(offset), outgoing(2 * offset)])
        first_arrived = from_behind(stacked, "section", offset)
        second_arrived = from_behind(first_arrived[1:2], "section", offset)
        arrivals.append((offset, first_arrived[0]))
        arrivals.append((2 * offset, second_arrived[0]))
    hidden = outgoing(0)
    for offset, arrived in arrivals:
        hidden = jnp.where(needed == offset, arrived, hidden)
    return hidden


def send_to(here):
    return 2 - 2 * here + 5 * (here // 2)


def taken_from(here):
    return 1 + 2 * here - 5 * (here // 2)


def pick_kernel(map_ref, bounds_ref, counts_ref, teacher_ref, slab_ref, count_ref, sem):
    here = lax.axis_index("section")
    place = map_ref[send_to(here)] - bounds_ref[here]
    place = jnp.minimum(jnp.maximum(place, 0), teacher_ref.shape[0] - 1)
    copy = pltpu.make_async_copy(teacher_ref.at[place], slab_ref, sem)
    copy.start()
    count_ref[...] = jnp.full(count_ref.shape, counts_ref[0].astype(F32), F32)
    copy.wait()


def pick(teacher_states, layer_map, boundaries, valid_counts, width):
    smem = pl.BlockSpec(memory_space=pltpu.SMEM)
    vmem = pl.BlockSpec(memory_space=pltpu.VMEM)
    return pl.pallas_call(
        pick_kernel,
        out_shape=(
            jax.ShapeDtypeStruct(teacher_states.shape[1:], BF16),
            jax.ShapeDtypeStruct((8, width), F32),
        ),
        in_specs=[smem, smem, smem, pl.BlockSpec(memory_space=pl.ANY)],
        out_specs=(vmem, vmem),
        scratch_shapes=[pltpu.SemaphoreType.DMA],
    )(layer_map, boundaries, valid_counts, teacher_states)


def main_kernel(n, direct, s_hbm, slab_hbm, w_hbm, count_ref, sg_ref, pg_hbm, loss_ref,
                slab_ref, weights, stud, normed, tgt, proj, scaled, own, part_a, part_b, got_a, got_b,
                counts, losses, loss_out, pg,
                in_sem, slab_sem, w_sem, ag_send, ag_recv, t_send, t_recv, rs_send, rs_recv,
                c_send, c_recv, l_send, l_recv, pg_sem):
    here = lax.axis_index("section")
    me = lax.axis_index("dp")
    rows, ds_width = s_hbm.shape
    width = weights.shape[1]
    half = rows // CHUNKS
    steps_a, steps_b = n // 2, n - 1 - n // 2
    teacher_width = width * n

    x, z = me % 2, me // 2
    position = z * (1 - x) + (n - 1 - z) * x
    sign = 1 - 2 * (here % 2)

    def at(offset):
        p = (position + sign * offset + 2 * n) % n
        low = 1 - p // (n // 2)
        return low * (2 * p) + (1 - low) * (2 * (n - 1 - p) + 1)

    after, before = at(1), at(-1)

    def block(index):
        return pl.ds(pl.multiple_of(index * rows, rows), rows)

    load_students = pltpu.make_async_copy(s_hbm, stud.at[block(me)], in_sem)
    load_students.start()
    load_slab = pltpu.make_async_copy(slab_hbm, slab_ref, slab_sem)
    load_slab.start()
    barrier = pltpu.get_barrier_semaphore()
    for k in range(1, n):
        pl.semaphore_signal(barrier, inc=1, device_id=(here, (me + k) % n), device_id_type=MESH)
    expected = n - 1
    if direct:
        for k in range(n):
            pl.semaphore_signal(barrier, inc=1, device_id=(send_to(here), (me + k) % n), device_id_type=MESH)
            pl.semaphore_signal(barrier, inc=1, device_id=(taken_from(here), (me + k) % n), device_id_type=MESH)
        expected += 2 * n
    load_weights = pltpu.make_async_copy(w_hbm, weights, w_sem)
    load_weights.start()
    pl.semaphore_wait(barrier, expected)
    load_students.wait()

    def ag_copy(direction, step, chunk):
        offset = -step if direction == 0 else step
        index = at(offset)
        piece = pl.ds(pl.multiple_of(index * rows + chunk * half, half), half)
        return pltpu.make_async_remote_copy(
            src_ref=stud.at[piece], dst_ref=stud.at[piece],
            send_sem=ag_send.at[direction, step, chunk], recv_sem=ag_recv.at[direction, step, chunk],
            device_id=(here, after if direction == 0 else before), device_id_type=MESH)

    def ag_arrival(direction, step, chunk):
        index = at(-(step + 1) if direction == 0 else step + 1)
        piece = stud.at[pl.ds(pl.multiple_of(index * rows + chunk * half, half), half)]
        return pltpu.make_async_remote_copy(
            src_ref=piece, dst_ref=piece,
            send_sem=ag_send.at[direction, step, chunk], recv_sem=ag_recv.at[direction, step, chunk],
            device_id=(here, before), device_id_type=MESH)

    ag_steps = (steps_a, steps_b)
    sent = []

    def go(copy):
        copy.start()
        sent.append(copy)

    for chunk in range(CHUNKS):
        for direction in range(2):
            if ag_steps[direction] > 0:
                go(ag_copy(direction, 0, chunk))

    def small(source, slots, send_sems, recv_sems, k):
        peer = (me + k) % n
        return pltpu.make_async_remote_copy(
            src_ref=source, dst_ref=slots.at[me], send_sem=send_sems.at[k], recv_sem=recv_sems.at[me],
            device_id=(here, peer), device_id_type=MESH)

    def small_arrival(slots, send_sems, recv_sems, k):
        peer = (me + k) % n
        return pltpu.make_async_remote_copy(
            src_ref=slots.at[peer], dst_ref=slots.at[peer], send_sem=send_sems.at[k],
            recv_sem=recv_sems.at[peer], device_id=(here, peer), device_id_type=MESH)

    for k in range(1, n):
        go(small(count_ref, counts, c_send, c_recv, k))
    counts[me] = count_ref[...]

    load_slab.wait()
    squares = jnp.zeros((rows, 1), F32)
    for g in range(n):
        h = slab_ref[:, g * width:(g + 1) * width].astype(F32)
        squares += jnp.sum(h * h, axis=1, keepdims=True)
    inverse = lax.rsqrt(squares / teacher_width + norm_eps)
    for g in range(n):
        h = slab_ref[:, g * width:(g + 1) * width].astype(F32)
        normed[g] = (h * inverse).astype(BF16)
    taker = send_to(here) if direct else here

    def target_copy(offset):
        g = at(offset)
        return pltpu.make_async_remote_copy(
            src_ref=normed.at[g], dst_ref=tgt.at[block(me)], send_sem=t_send.at[g], recv_sem=t_recv.at[me],
            device_id=(taker, g), device_id_type=MESH)

    def target_arrival(index):
        return pltpu.make_async_remote_copy(
            src_ref=tgt.at[block(index)], dst_ref=tgt.at[block(index)], send_sem=t_send.at[index],
            recv_sem=t_recv.at[index], device_id=(taker, index), device_id_type=MESH)

    far_first = [steps_a]
    for k in range(steps_b, 0, -1):
        far_first += [k, -k]
    if direct:
        far_first.append(0)
    else:
        tgt[block(me), :] = normed[me]
    for offset in far_first[:3]:
        go(target_copy(offset))
    queue = far_first[3:]

    def project(index):
        proj[block(index), :] = jnp.dot(stud[block(index), :], weights[...], preferred_element_type=F32)

    row = lax.broadcasted_iota(jnp.int32, (rows, width), 0).astype(F32)
    losses[me] = jnp.zeros(losses.shape[1:], F32)

    def total():
        value = counts[0][0:1, :]
        for b in range(1, n):
            value = value + counts[b][0:1, :]
        return value

    def residual(offset):
        index = at(offset)
        if direct or offset != 0:
            target_arrival(index).wait_recv()
        left = proj[block(index), :] - tgt[block(index), :].astype(F32)
        valid = jnp.where(row < counts[index][0:1, :], 1.0, 0.0)
        kept = valid * left
        line = jnp.sum(kept * left, axis=0, keepdims=True)
        losses[me] += jnp.broadcast_to(line, losses.shape[1:])
        scaled[block(index), :] = (loss_scale / total() * kept).astype(BF16)

    def share(offset, into):
        own[into] = lax.dot_general(
            scaled[block(at(offset)), :], weights[...], (((1,), (1,)), ((), ())), preferred_element_type=F32)

    def rs_copy(direction, step, chunk):
        parts, gots = (part_a, got_a) if direction == 0 else (part_b, got_b)
        piece = pl.ds(chunk * half, half)
        return pltpu.make_async_remote_copy(
            src_ref=parts.at[step, piece], dst_ref=gots.at[step, piece],
            send_sem=rs_send.at[direction, step, chunk], recv_sem=rs_recv.at[direction, step, chunk],
            device_id=(here, after if direction == 0 else before), device_id_type=MESH)

    def grad_tile(tile):
        size = ds_width // GRAD_TILES
        left = stud[:, tile * size:(tile + 1) * size]
        pg[tile * size:(tile + 1) * size, :] = lax.dot_general(
            left, scaled[...], (((0,), (0,)), ((), ())), preferred_element_type=F32).astype(BF16)
        piece = pl.ds(tile * size, size)
        go_local = pltpu.make_async_copy(pg.at[piece], pg_hbm.at[piece], pg_sem.at[tile])
        go_local.start()
        return go_local

    def advance(step, directions):
        for chunk in range(CHUNKS):
            piece = slice(chunk * half, (chunk + 1) * half)
            for direction in directions:
                if step >= ag_steps[direction]:
                    continue
                parts, gots = (part_a, got_a) if direction == 0 else (part_b, got_b)
                value = own[direction, piece, :]
                if step > 0:
                    rs_copy(direction, step - 1, chunk).wait_recv()
                    value = value + gots[step - 1, piece, :].astype(F32)
                parts[step, piece, :] = value.astype(BF16)
                go(rs_copy(direction, step, chunk))

    def prepare(step, direction):
        if step < ag_steps[direction]:
            offset = steps_a - step if direction == 0 else step - steps_b
            residual(offset)
            share(offset, direction)

    load_weights.wait()
    project(me)
    for step in range(steps_a):
        if step == steps_a - 1:
            prepare(0, 1)
            advance(0, (1,))
        for chunk in range(CHUNKS):
            for direction in range(2):
                if step < ag_steps[direction]:
                    ag_arrival(direction, step, chunk).wait_recv()
                    if step + 1 < ag_steps[direction]:
                        go(ag_copy(direction, step + 1, chunk))
        for offset in queue[:2]:
            go(target_copy(offset))
        queue = queue[2:]
        if step == 0:
            for k in range(1, n):
                small_arrival(counts, c_send, c_recv, k).wait_recv()
        project(at(-(step + 1)))
        if step < steps_b:
            project(at(step + 1))
    for offset in queue:
        go(target_copy(offset))

    prepare(0, 0)
    advance(0, (0,))
    for step in range(1, steps_a):
        prepare(step, 1)
        prepare(step, 0)
        if step == steps_a - 1:
            residual(0)
            share(0, 1)
        advance(step, (1, 0))

    line = losses[me][0:1, :]
    folded = jnp.sum(line, axis=1, keepdims=True)
    loss_out[me] = jnp.broadcast_to(folded, loss_out.shape[1:])
    written = [grad_tile(0)]
    for k in range(1, n):
        go(small(loss_out.at[me], loss_out, l_send, l_recv, k))
    for tile in range(1, GRAD_TILES):
        written.append(grad_tile(tile))

    for k in range(1, n):
        small_arrival(loss_out, l_send, l_recv, k).wait_recv()
    whole = loss_out[0][0:1, :]
    count = total()[:, 0:128]
    for b in range(1, n):
        whole = whole + loss_out[b][0:1, :]
    loss_ref[...] = jnp.broadcast_to(whole / (count * teacher_width), loss_ref.shape)

    for chunk in range(CHUNKS):
        piece = slice(chunk * half, (chunk + 1) * half)
        value = own[1, piece, :]
        rs_copy(0, steps_a - 1, chunk).wait_recv()
        value = value + got_a[steps_a - 1, piece, :].astype(F32)
        if steps_b > 0:
            rs_copy(1, steps_b - 1, chunk).wait_recv()
            value = value + got_b[steps_b - 1, piece, :].astype(F32)
        sg_ref[piece, :] = value.astype(BF16)
    for copy in written:
        copy.wait()
    for copy in sent:
        copy.wait_send()


def per_device(student_states, teacher_states, projector, layer_map, boundaries, valid_counts):
    n = lax.axis_size("dp")
    rows, ds_width = student_states.shape[1:]
    width = projector.shape[2]
    direct = lax.axis_size("section") == 4
    if direct:
        slab, count = pick(teacher_states, layer_map, boundaries, valid_counts, width)
    else:
        slab = relayed(teacher_states, layer_map, boundaries)
        count = jnp.full((8, width), valid_counts[0].astype(F32), F32)
    steps_a, steps_b = n // 2, n - 1 - n // 2
    vmem = pl.BlockSpec(memory_space=pltpu.VMEM)
    anywhere = pl.BlockSpec(memory_space=pl.ANY)
    dma = pltpu.SemaphoreType.DMA
    student_grad, projector_grad, loss = pl.pallas_call(
        functools.partial(main_kernel, n, direct),
        out_shape=(
            jax.ShapeDtypeStruct((rows, ds_width), BF16),
            jax.ShapeDtypeStruct((ds_width, width), BF16),
            jax.ShapeDtypeStruct((8, 128), F32),
        ),
        in_specs=[anywhere, anywhere, anywhere, vmem],
        out_specs=(vmem, anywhere, vmem),
        scratch_shapes=[
            pltpu.VMEM((rows, n * width), BF16),
            pltpu.VMEM((ds_width, width), BF16),
            pltpu.VMEM((n * rows, ds_width), BF16),
            pltpu.VMEM((n, rows, width), BF16),
            pltpu.VMEM((n * rows, width), BF16),
            pltpu.VMEM((n * rows, width), F32),
            pltpu.VMEM((n * rows, width), BF16),
            pltpu.VMEM((2, rows, ds_width), F32),
            pltpu.VMEM((steps_a, rows, ds_width), BF16),
            pltpu.VMEM((max(steps_b, 1), rows, ds_width), BF16),
            pltpu.VMEM((steps_a, rows, ds_width), BF16),
            pltpu.VMEM((max(steps_b, 1), rows, ds_width), BF16),
            pltpu.VMEM((n, 8, width), F32),
            pltpu.VMEM((n, 8, width), F32),
            pltpu.VMEM((n, 8, 128), F32),
            pltpu.VMEM((ds_width, width), BF16),
            dma,
            dma,
            dma,
            dma((2, steps_a, CHUNKS)),
            dma((2, steps_a, CHUNKS)),
            dma((n,)),
            dma((n,)),
            dma((2, steps_a, CHUNKS)),
            dma((2, steps_a, CHUNKS)),
            dma((n,)),
            dma((n,)),
            dma((n,)),
            dma((n,)),
            dma((GRAD_TILES,)),
        ],
        compiler_params=pltpu.CompilerParams(
            collective_id=0, has_side_effects=True, vmem_limit_bytes=56 * 1024 * 1024
        ),
    )(student_states[0], slab, projector[0], count)
    return student_grad[None], projector_grad[None], loss[0, 0:1]


def solution(mesh):
    in_specs = (
        P("section", "dp", None),
        P("section", "dp", None),
        P("section", None, "dp"),
        P(),
        P(),
        P("dp"),
    )
    out_specs = (P("section", "dp", None), P("section", None, "dp"), P("section"))
    return jax.shard_map(
        per_device, mesh=mesh, in_specs=in_specs, out_specs=out_specs, check_vma=False
    )
```

profile of v0, /device:TPU:0, one launch (start us, length us, event | category | flops | bytes accessed | tf_op | source)
XLA Modules:
  0.0 146.5 jit_solution(14690389189394323453)
XLA Ops:
  1.3 3.4 %shard_map.85 = (bf16[128,7168]{1,0:T(8,128)(2,1)}, f32[8,896]{1,0:T(8,128)}) custom-call(s32[4]{0:T(128)} %map_ref.1, s32[5]{0:T(128)} %bounds_ref.1, s32[1]{0:T(128)S(6)} %copy.11.counts_ref, bf16[4,128,7168]{2,1,0:T(8,128)(2,1)} %teacher_ref.1), custom_call_target="tpu_custom_call" | custom-call | tf_op jit(solution)/shard_map/pallas_call | solution.py:81
  4.7 134.5 %shard_map.86 = (bf16[128,2048]{1,0:T(8,128)(2,1)}, bf16[2048,896]{1,0:T(8,128)(2,1)}, f32[8,128]{1,0:T(8,128)}) custom-call(bf16[128,2048]{1,0:T(8,128)(2,1)} %bitcast.8, bf16[128,7168]{1,0:T(8,128)(2,1)} %get-tuple-element.8.slab_hbm, bf16[2048,896]{1,0:T(8,128)(2,1)} %bitcast.6, f32[8,896]{1,0:T(8,128)} %get-tuple-element.9.count_ref), custom_call_target="tpu_custom_call" | custom-call | tf_op jit(solution)/shard_map/pallas_call | solution.py:361
  139.3 1.2 slice.3
  140.4 1.9 %copy.12 = bf16[1,128,2048]{2,1,0:T(8,128)(2,1)} copy(bf16[1,128,2048]{2,1,0:T(8,128)(2,1)} %bitcast.7) | data formatting | bytes 1048576
  142.3 4.2 %copy.13 = bf16[1,2048,896]{2,1,0:T(8,128)(2,1)} copy(bf16[1,2048,896]{2,1,0:T(8,128)(2,1)} %bitcast.5) | data formatting | bytes 7340032
where the time goes:
time: 147 us; the launch traced here: 146 us
  Pallas kernels  138 us (94%)
  local copies, waits for them, and re-layouts  7.23 us (5%)
    pallas_call x1, Pallas kernels, per_device(): pl.pallas_call(functools.partial(main_kernel, n, direct), out_shape=(jax....  135 us
    unnamed x2, local copies, waits for them, and re-layouts  6.05 us
    pallas_call x1, Pallas kernels, pick(): pl.pallas_call(pick_kernel, out_shape=(jax.ShapeDtypeStruct(teacher_state...  3.43 us

commit v1 on v0

--- a/solution.py
+++ b/solution.py
@@ -75,14 +75,14 @@
     copy.wait()
 
 
-def pick(teacher_states, layer_map, boundaries, valid_counts, width):
+def pick(teacher_states, layer_map, boundaries, valid_counts):
     smem = pl.BlockSpec(memory_space=pltpu.SMEM)
     vmem = pl.BlockSpec(memory_space=pltpu.VMEM)
     return pl.pallas_call(
         pick_kernel,
         out_shape=(
             jax.ShapeDtypeStruct(teacher_states.shape[1:], BF16),
-            jax.ShapeDtypeStruct((8, width), F32),
+            jax.ShapeDtypeStruct((8, 128), F32),
         ),
         in_specs=[smem, smem, smem, pl.BlockSpec(memory_space=pl.ANY)],
         out_specs=(vmem, vmem),
@@ -94,7 +94,7 @@
                 slab_ref, weights, stud, normed, tgt, proj, scaled, own, part_a, part_b, got_a, got_b,
                 counts, losses, loss_out, pg,
                 in_sem, slab_sem, w_sem, ag_send, ag_recv, t_send, t_recv, rs_send, rs_recv,
-                c_send, c_recv, l_send, l_recv, pg_sem):
+                c_send, c_recv, l_send, l_recv, pg_sem, passing, p_send, p_recv):
     here = lax.axis_index("section")
     me = lax.axis_index("dp")
     rows, ds_width = s_hbm.shape
@@ -135,34 +135,70 @@
     pl.semaphore_wait(barrier, expected)
     load_students.wait()
 
-    def ag_copy(direction, step, chunk):
-        offset = -step if direction == 0 else step
-        index = at(offset)
-        piece = pl.ds(pl.multiple_of(index * rows + chunk * half, half), half)
-        return pltpu.make_async_remote_copy(
-            src_ref=stud.at[piece], dst_ref=stud.at[piece],
-            send_sem=ag_send.at[direction, step, chunk], recv_sem=ag_recv.at[direction, step, chunk],
-            device_id=(here, after if direction == 0 else before), device_id_type=MESH)
-
-    def ag_arrival(direction, step, chunk):
-        index = at(-(step + 1) if direction == 0 else step + 1)
-        piece = stud.at[pl.ds(pl.multiple_of(index * rows + chunk * half, half), half)]
-        return pltpu.make_async_remote_copy(
-            src_ref=piece, dst_ref=piece,
-            send_sem=ag_send.at[direction, step, chunk], recv_sem=ag_recv.at[direction, step, chunk],
-            device_id=(here, before), device_id_type=MESH)
+    pair, line = me % 2, me // 2
+    partner = me + 1 - 2 * pair
+    lines = n // 2
+
+    def reached(place):
+        return (line + lines - place) // lines
+
+    def arrival_of(k):
+        value = 0
+        for place in range(lines):
+            order = []
+            for step in range(lines - 1):
+                order += [b for b in (place - 1 - step, place + 1 + step) if 0 <= b < lines]
+            value = value + order[k] * (reached(place) - reached(place + 1))
+        return value
+
+    def piece_of(index, chunk):
+        return stud.at[pl.ds(pl.multiple_of(index * rows + chunk * half, half), half)]
+
+    UP, DOWN, ACROSS = 0, 1, 2
+    targets_of = (me + 2, me - 2, me + 1 - 2 * pair)
+
+    def ag_copy(way, index, step, chunk):
+        return pltpu.make_async_remote_copy(
+            src_ref=piece_of(index, chunk), dst_ref=piece_of(index, chunk),
+            send_sem=ag_send.at[way, step, chunk], recv_sem=ag_recv.at[index, chunk],
+            device_id=(here, targets_of[way]), device_id_type=MESH)
+
+    def ag_arrival(index, chunk):
+        return pltpu.make_async_remote_copy(
+            src_ref=piece_of(index, chunk), dst_ref=piece_of(index, chunk),
+            send_sem=ag_send.at[0, 0, chunk], recv_sem=ag_recv.at[index, chunk],
+            device_id=(here, targets_of[2]), device_id_type=MESH)
 
     ag_steps = (steps_a, steps_b)
     sent = []
+    sent_if = []
 
     def go(copy):
         copy.start()
         sent.append(copy)
 
+    def go_if(condition, copy):
+        pl.when(condition)(copy.start)
+        sent_if.append((condition, copy))
+
+    can_up, can_down = line < lines - 1, line > 0
     for chunk in range(CHUNKS):
-        for direction in range(2):
-            if ag_steps[direction] > 0:
-                go(ag_copy(direction, 0, chunk))
+        go_if(can_up, ag_copy(UP, me, 0, chunk))
+        go_if(can_down, ag_copy(DOWN, me, 0, chunk))
+        go(ag_copy(ACROSS, me, 0, chunk))
+
+    def relay(step):
+        below, above = me - 2 - 2 * step, me + 2 + 2 * step
+        from_below, from_above = line - 1 - step >= 0, line + 1 + step < lines
+        for chunk in range(CHUNKS):
+            pl.when(from_below)(ag_arrival(below, chunk).wait_recv)
+            go_if(from_below & can_up, ag_copy(UP, below, step + 1, chunk))
+            pl.when(from_above)(ag_arrival(above, chunk).wait_recv)
+            go_if(from_above & can_down, ag_copy(DOWN, above, step + 1, chunk))
+        for chunk in range(CHUNKS):
+            go_if(from_below, ag_copy(ACROSS, below, 2 * step + 1, chunk))
+        for chunk in range(CHUNKS):
+            go_if(from_above, ag_copy(ACROSS, above, 2 * step + 2, chunk))
 
     def small(source, slots, send_sems, recv_sems, k):
         peer = (me + k) % n
@@ -191,32 +227,42 @@
         normed[g] = (h * inverse).astype(BF16)
     taker = send_to(here) if direct else here
 
-    def target_copy(offset):
-        g = at(offset)
-        return pltpu.make_async_remote_copy(
-            src_ref=normed.at[g], dst_ref=tgt.at[block(me)], send_sem=t_send.at[g], recv_sem=t_recv.at[me],
+    def target_copy(source, owner, g):
+        return pltpu.make_async_remote_copy(
+            src_ref=source, dst_ref=tgt.at[block(owner)], send_sem=t_send.at[owner, g], recv_sem=t_recv.at[owner],
             device_id=(taker, g), device_id_type=MESH)
 
+    def crossing(k):
+        g = 2 * ((line + k) % lines) + 1 - pair
+        return pltpu.make_async_remote_copy(
+            src_ref=normed.at[g], dst_ref=passing.at[k], send_sem=p_send.at[k], recv_sem=p_recv.at[k],
+            device_id=(here, partner), device_id_type=MESH)
+
+    def own_target(k):
+        g = 2 * ((line + k) % lines) + pair
+        return target_copy(normed.at[g], me, g)
+
+    def passed_target(k):
+        g = 2 * ((line + k) % lines) + pair
+        return target_copy(passing.at[k], partner, g)
+
     def target_arrival(index):
         return pltpu.make_async_remote_copy(
-            src_ref=tgt.at[block(index)], dst_ref=tgt.at[block(index)], send_sem=t_send.at[index],
+            src_ref=tgt.at[block(index)], dst_ref=tgt.at[block(index)], send_sem=t_send.at[0, index],
             recv_sem=t_recv.at[index], device_id=(taker, index), device_id_type=MESH)
 
-    far_first = [steps_a]
-    for k in range(steps_b, 0, -1):
-        far_first += [k, -k]
+    if not direct:
+        tgt[block(me), :] = normed[me]
+    for k in range(1, lines):
+        go(crossing(k))
+    go(target_copy(normed.at[partner], me, partner))
     if direct:
-        far_first.append(0)
-    else:
-        tgt[block(me), :] = normed[me]
-    for offset in far_first[:3]:
-        go(target_copy(offset))
-    queue = far_first[3:]
+        go(own_target(0))
 
     def project(index):
         proj[block(index), :] = jnp.dot(stud[block(index), :], weights[...], preferred_element_type=F32)
 
-    row = lax.broadcasted_iota(jnp.int32, (rows, width), 0).astype(F32)
+    row = lax.broadcasted_iota(jnp.int32, (rows, 1), 0).astype(F32)
     losses[me] = jnp.zeros(losses.shape[1:], F32)
 
     def total():
@@ -230,11 +276,11 @@
         if direct or offset != 0:
             target_arrival(index).wait_recv()
         left = proj[block(index), :] - tgt[block(index), :].astype(F32)
-        valid = jnp.where(row < counts[index][0:1, :], 1.0, 0.0)
+        valid = jnp.where(row < counts[index][0:1, 0:1], 1.0, 0.0)
         kept = valid * left
         line = jnp.sum(kept * left, axis=0, keepdims=True)
         losses[me] += jnp.broadcast_to(line, losses.shape[1:])
-        scaled[block(index), :] = (loss_scale / total() * kept).astype(BF16)
+        scaled[block(index), :] = (loss_scale / total()[:, 0:1] * kept).astype(BF16)
 
     def share(offset, into):
         own[into] = lax.dot_general(
@@ -278,30 +324,33 @@
             residual(offset)
             share(offset, direction)
 
+    def project_across(source):
+        index = 2 * source + 1 - pair
+        for chunk in range(CHUNKS):
+            ag_arrival(index, chunk).wait_recv()
+        project(index)
+
     load_weights.wait()
     project(me)
-    for step in range(steps_a):
-        if step == steps_a - 1:
-            prepare(0, 1)
-            advance(0, (1,))
-        for chunk in range(CHUNKS):
-            for direction in range(2):
-                if step < ag_steps[direction]:
-                    ag_arrival(direction, step, chunk).wait_recv()
-                    if step + 1 < ag_steps[direction]:
-                        go(ag_copy(direction, step + 1, chunk))
-        for offset in queue[:2]:
-            go(target_copy(offset))
-        queue = queue[2:]
+    for step in range(lines - 1):
+        relay(step)
+        if step == min(1, lines - 2):
+            for k in range(lines - 1, 0, -1):
+                go(own_target(k))
+        project(2 * arrival_of(step) + pair)
         if step == 0:
             for k in range(1, n):
                 small_arrival(counts, c_send, c_recv, k).wait_recv()
-        project(at(-(step + 1)))
-        if step < steps_b:
-            project(at(step + 1))
-    for offset in queue:
-        go(target_copy(offset))
-
+            project_across(line)
+        if step == min(1, lines - 2):
+            for k in range(1, lines):
+                crossing(k).wait_recv()
+                go(passed_target(k))
+    for step in range(lines - 1):
+        project_across(arrival_of(step))
+
+    prepare(0, 1)
+    advance(0, (1,))
     prepare(0, 0)
     advance(0, (0,))
     for step in range(1, steps_a):
@@ -324,7 +373,7 @@
     for k in range(1, n):
         small_arrival(loss_out, l_send, l_recv, k).wait_recv()
     whole = loss_out[0][0:1, :]
-    count = total()[:, 0:128]
+    count = total()
     for b in range(1, n):
         whole = whole + loss_out[b][0:1, :]
     loss_ref[...] = jnp.broadcast_to(whole / (count * teacher_width), loss_ref.shape)
@@ -342,6 +391,8 @@
         copy.wait()
     for copy in sent:
         copy.wait_send()
+    for condition, copy in sent_if:
+        pl.when(condition)(copy.wait_send)
 
 
 def per_device(student_states, teacher_states, projector, layer_map, boundaries, valid_counts):
@@ -350,10 +401,10 @@
     width = projector.shape[2]
     direct = lax.axis_size("section") == 4
     if direct:
-        slab, count = pick(teacher_states, layer_map, boundaries, valid_counts, width)
+        slab, count = pick(teacher_states, layer_map, boundaries, valid_counts)
     else:
         slab = relayed(teacher_states, layer_map, boundaries)
-        count = jnp.full((8, width), valid_counts[0].astype(F32), F32)
+        count = jnp.full((8, 128), valid_counts[0].astype(F32), F32)
     steps_a, steps_b = n // 2, n - 1 - n // 2
     vmem = pl.BlockSpec(memory_space=pltpu.VMEM)
     anywhere = pl.BlockSpec(memory_space=pl.ANY)
@@ -380,16 +431,16 @@
             pltpu.VMEM((max(steps_b, 1), rows, ds_width), BF16),
             pltpu.VMEM((steps_a, rows, ds_width), BF16),
             pltpu.VMEM((max(steps_b, 1), rows, ds_width), BF16),
-            pltpu.VMEM((n, 8, width), F32),
+            pltpu.VMEM((n, 8, 128), F32),
             pltpu.VMEM((n, 8, width), F32),
             pltpu.VMEM((n, 8, 128), F32),
             pltpu.VMEM((ds_width, width), BF16),
             dma,
             dma,
             dma,
-            dma((2, steps_a, CHUNKS)),
-            dma((2, steps_a, CHUNKS)),
-            dma((n,)),
+            dma((3, n, CHUNKS)),
+            dma((n, CHUNKS)),
+            dma((n, n)),
             dma((n,)),
             dma((2, steps_a, CHUNKS)),
             dma((2, steps_a, CHUNKS)),
@@ -398,6 +449,9 @@
             dma((n,)),
             dma((n,)),
             dma((GRAD_TILES,)),
+            pltpu.VMEM((n // 2, rows, width), BF16),
+            dma((n // 2,)),
+            dma((n // 2,)),
         ],
         compiler_params=pltpu.CompilerParams(
             collective_id=0, has_side_effects=True, vmem_limit_bytes=56 * 1024 * 1024

time: 147 us -> 132 us (0.90)
  Pallas kernels: 138 us -> 123 us
    pallas_call x1, Pallas kernels: 135 us -> 120 us  [per_device(): pl.pallas_call(functools.partial(main_kernel, n, direct), out_shape=(jax....]
where the time goes in v1:
time: 132 us
  Pallas kernels  123 us (93%)
  local copies, waits for them, and re-layouts  7.23 us (5%)
    pallas_call x1, Pallas kernels, per_device(): pl.pallas_call(functools.partial(main_kernel, n, direct), out_shape=(jax....  120 us
    unnamed x2, local copies, waits for them, and re-layouts  6.05 us
    pallas_call x1, Pallas kernels, pick(): pl.pallas_call(pick_kernel, out_shape=(jax.ShapeDtypeStruct(teacher_state...  3.43 us

profile of v1, /device:TPU:0, one launch (start us, length us, event | category | flops | bytes accessed | tf_op | source)
XLA Modules:
  0.0 131.9 jit_solution(10614421349842311160)
XLA Ops:
  1.3 3.4 %shard_map.85 = (bf16[128,7168]{1,0:T(8,128)(2,1)}, f32[8,128]{1,0:T(8,128)}) custom-call(s32[4]{0:T(128)} %map_ref.1, s32[5]{0:T(128)} %bounds_ref.1, s32[1]{0:T(128)S(6)} %copy.11.counts_ref, bf16[4,128,7168]{2,1,0:T(8,128)(2,1)} %teacher_ref.1), custom_call_target="tpu_custom_call" | custom-call | tf_op jit(solution)/shard_map/pallas_call | solution.py:81
  4.7 119.9 %shard_map.86 = (bf16[128,2048]{1,0:T(8,128)(2,1)}, bf16[2048,896]{1,0:T(8,128)(2,1)}, f32[8,128]{1,0:T(8,128)}) custom-call(bf16[128,2048]{1,0:T(8,128)(2,1)} %bitcast.7, bf16[128,7168]{1,0:T(8,128)(2,1)} %get-tuple-element.8.slab_hbm, bf16[2048,896]{1,0:T(8,128)(2,1)} %bitcast.5, f32[8,128]{1,0:T(8,128)} %get-tuple-element.9.count_ref), custom_call_target="tpu_custom_call" | custom-call | tf_op jit(solution)/shard_map/pallas_call | solution.py:412
  124.7 1.2 slice.3
  125.9 1.9 %copy.12 = bf16[1,128,2048]{2,1,0:T(8,128)(2,1)} copy(bf16[1,128,2048]{2,1,0:T(8,128)(2,1)} %bitcast.8) | data formatting | bytes 1048576
  127.7 4.2 %copy.13 = bf16[1,2048,896]{2,1,0:T(8,128)(2,1)} copy(bf16[1,2048,896]{2,1,0:T(8,128)(2,1)} %bitcast.6) | data formatting | bytes 7340032

commit v2 on v1

--- a/solution.py
+++ b/solution.py
@@ -65,36 +65,11 @@
     return 1 + 2 * here - 5 * (here // 2)
 
 
-def pick_kernel(map_ref, bounds_ref, counts_ref, teacher_ref, slab_ref, count_ref, sem):
-    here = lax.axis_index("section")
-    place = map_ref[send_to(here)] - bounds_ref[here]
-    place = jnp.minimum(jnp.maximum(place, 0), teacher_ref.shape[0] - 1)
-    copy = pltpu.make_async_copy(teacher_ref.at[place], slab_ref, sem)
-    copy.start()
-    count_ref[...] = jnp.full(count_ref.shape, counts_ref[0].astype(F32), F32)
-    copy.wait()
-
-
-def pick(teacher_states, layer_map, boundaries, valid_counts):
-    smem = pl.BlockSpec(memory_space=pltpu.SMEM)
-    vmem = pl.BlockSpec(memory_space=pltpu.VMEM)
-    return pl.pallas_call(
-        pick_kernel,
-        out_shape=(
-            jax.ShapeDtypeStruct(teacher_states.shape[1:], BF16),
-            jax.ShapeDtypeStruct((8, 128), F32),
-        ),
-        in_specs=[smem, smem, smem, pl.BlockSpec(memory_space=pl.ANY)],
-        out_specs=(vmem, vmem),
-        scratch_shapes=[pltpu.SemaphoreType.DMA],
-    )(layer_map, boundaries, valid_counts, teacher_states)
-
-
-def main_kernel(n, direct, s_hbm, slab_hbm, w_hbm, count_ref, sg_ref, pg_hbm, loss_ref,
-                slab_ref, weights, stud, normed, tgt, proj, scaled, own, part_a, part_b, got_a, got_b,
-                counts, losses, loss_out, pg,
+def main_kernel(n, direct, map_ref, bounds_ref, counts_ref, s_hbm, t_hbm, w_hbm, sg_ref, pg, loss_ref,
+                teacher, count_ref, weights, stud, normed, tgt, proj, scaled, own, part_a, part_b, got_a, got_b,
+                counts, losses, loss_out,
                 in_sem, slab_sem, w_sem, ag_send, ag_recv, t_send, t_recv, rs_send, rs_recv,
-                c_send, c_recv, l_send, l_recv, pg_sem, passing, p_send, p_recv):
+                c_send, c_recv, l_send, l_recv, passing, p_send, p_recv):
     here = lax.axis_index("section")
     me = lax.axis_index("dp")
     rows, ds_width = s_hbm.shape
@@ -119,8 +94,10 @@
 
     load_students = pltpu.make_async_copy(s_hbm, stud.at[block(me)], in_sem)
     load_students.start()
-    load_slab = pltpu.make_async_copy(slab_hbm, slab_ref, slab_sem)
-    load_slab.start()
+    held = teacher.shape[0]
+    load_teacher = [
+        pltpu.make_async_copy(t_hbm.at[slot], teacher.at[slot], slab_sem.at[slot]) for slot in range(held)
+    ]
     barrier = pltpu.get_barrier_semaphore()
     for k in range(1, n):
         pl.semaphore_signal(barrier, inc=1, device_id=(here, (me + k) % n), device_id_type=MESH)
@@ -131,7 +108,10 @@
             pl.semaphore_signal(barrier, inc=1, device_id=(taken_from(here), (me + k) % n), device_id_type=MESH)
         expected += 2 * n
     load_weights = pltpu.make_async_copy(w_hbm, weights, w_sem)
+    for copy in load_teacher:
+        copy.start()
     load_weights.start()
+    count_ref[...] = jnp.full(count_ref.shape, counts_ref[0].astype(F32), F32)
     pl.semaphore_wait(barrier, expected)
     load_students.wait()
 
@@ -216,14 +196,18 @@
         go(small(count_ref, counts, c_send, c_recv, k))
     counts[me] = count_ref[...]
 
-    load_slab.wait()
+    for copy in load_teacher:
+        copy.wait()
+    place = 0
+    if direct:
+        place = jnp.clip(map_ref[send_to(here)] - bounds_ref[here], 0, held - 1)
     squares = jnp.zeros((rows, 1), F32)
     for g in range(n):
-        h = slab_ref[:, g * width:(g + 1) * width].astype(F32)
+        h = teacher[place, :, g * width:(g + 1) * width].astype(F32)
         squares += jnp.sum(h * h, axis=1, keepdims=True)
     inverse = lax.rsqrt(squares / teacher_width + norm_eps)
     for g in range(n):
-        h = slab_ref[:, g * width:(g + 1) * width].astype(F32)
+        h = teacher[place, :, g * width:(g + 1) * width].astype(F32)
         normed[g] = (h * inverse).astype(BF16)
     taker = send_to(here) if direct else here
 
@@ -299,10 +283,6 @@
         left = stud[:, tile * size:(tile + 1) * size]
         pg[tile * size:(tile + 1) * size, :] = lax.dot_general(
             left, scaled[...], (((0,), (0,)), ((), ())), preferred_element_type=F32).astype(BF16)
-        piece = pl.ds(tile * size, size)
-        go_local = pltpu.make_async_copy(pg.at[piece], pg_hbm.at[piece], pg_sem.at[tile])
-        go_local.start()
-        return go_local
 
     def advance(step, directions):
         for chunk in range(CHUNKS):
@@ -364,11 +344,11 @@
     line = losses[me][0:1, :]
     folded = jnp.sum(line, axis=1, keepdims=True)
     loss_out[me] = jnp.broadcast_to(folded, loss_out.shape[1:])
-    written = [grad_tile(0)]
+    grad_tile(0)
     for k in range(1, n):
         go(small(loss_out.at[me], loss_out, l_send, l_recv, k))
     for tile in range(1, GRAD_TILES):
-        written.append(grad_tile(tile))
+        grad_tile(tile)
 
     for k in range(1, n):
         small_arrival(loss_out, l_send, l_recv, k).wait_recv()
@@ -387,8 +367,6 @@
             rs_copy(1, steps_b - 1, chunk).wait_recv()
             value = value + got_b[steps_b - 1, piece, :].astype(F32)
         sg_ref[piece, :] = value.astype(BF16)
-    for copy in written:
-        copy.wait()
     for copy in sent:
         copy.wait_send()
     for condition, copy in sent_if:
@@ -400,26 +378,24 @@
     rows, ds_width = student_states.shape[1:]
     width = projector.shape[2]
     direct = lax.axis_size("section") == 4
-    if direct:
-        slab, count = pick(teacher_states, layer_map, boundaries, valid_counts)
-    else:
-        slab = relayed(teacher_states, layer_map, boundaries)
-        count = jnp.full((8, 128), valid_counts[0].astype(F32), F32)
+    teacher = teacher_states if direct else relayed(teacher_states, layer_map, boundaries)[None]
     steps_a, steps_b = n // 2, n - 1 - n // 2
+    smem = pl.BlockSpec(memory_space=pltpu.SMEM)
     vmem = pl.BlockSpec(memory_space=pltpu.VMEM)
     anywhere = pl.BlockSpec(memory_space=pl.ANY)
     dma = pltpu.SemaphoreType.DMA
     student_grad, projector_grad, loss = pl.pallas_call(
         functools.partial(main_kernel, n, direct),
         out_shape=(
-            jax.ShapeDtypeStruct((rows, ds_width), BF16),
-            jax.ShapeDtypeStruct((ds_width, width), BF16),
-            jax.ShapeDtypeStruct((8, 128), F32),
+            pltpu.VMEM((rows, ds_width), BF16),
+            pltpu.VMEM((ds_width, width), BF16),
+            pltpu.VMEM((8, 128), F32),
         ),
-        in_specs=[anywhere, anywhere, anywhere, vmem],
-        out_specs=(vmem, anywhere, vmem),
+        in_specs=[smem, smem, smem, anywhere, anywhere, anywhere],
+        out_specs=(vmem, vmem, vmem),
         scratch_shapes=[
-            pltpu.VMEM((rows, n * width), BF16),
+            pltpu.VMEM(teacher.shape, BF16),
+            pltpu.VMEM((8, 128), F32),
             pltpu.VMEM((ds_width, width), BF16),
             pltpu.VMEM((n * rows, ds_width), BF16),
             pltpu.VMEM((n, rows, width), BF16),
@@ -434,9 +410,8 @@
             pltpu.VMEM((n, 8, 128), F32),
             pltpu.VMEM((n, 8, width), F32),
             pltpu.VMEM((n, 8, 128), F32),
-            pltpu.VMEM((ds_width, width), BF16),
             dma,
-            dma,
+            dma((teacher.shape[0],)),
             dma,
             dma((3, n, CHUNKS)),
             dma((n, CHUNKS)),
@@ -448,7 +423,6 @@
             dma((n,)),
             dma((n,)),
             dma((n,)),
-            dma((GRAD_TILES,)),
             pltpu.VMEM((n // 2, rows, width), BF16),
             dma((n // 2,)),
             dma((n // 2,)),
@@ -456,7 +430,7 @@
         compiler_params=pltpu.CompilerParams(
             collective_id=0, has_side_effects=True, vmem_limit_bytes=56 * 1024 * 1024
         ),
-    )(student_states[0], slab, projector[0], count)
+    )(layer_map, boundaries, valid_counts, student_states[0], teacher, projector[0])
     return student_grad[None], projector_grad[None], loss[0, 0:1]
 
 

time: 132 us -> 124 us (0.939)
  local copies, waits for them, and re-layouts: 7.23 us -> 3.14 us
  Pallas kernels: 123 us -> 119 us
    pallas_call x2 -> x1, Pallas kernels: 123 us -> 119 us  [per_device(): pl.pallas_call(functools.partial(main_kernel, n, direct), out_shape=(pltp...]
    unnamed x2, local copies, waits for them, and re-layouts: 6.05 us -> 2.63 us
where the time goes in v2:
time: 124 us
  Pallas kernels  119 us (96%)
  local copies, waits for them, and re-layouts  3.14 us (3%)
  between operations  1.29 us (1%)
    pallas_call x1, Pallas kernels, per_device(): pl.pallas_call(functools.partial(main_kernel, n, direct), out_shape=(pltp...  119 us
    unnamed x2, local copies, waits for them, and re-layouts  2.63 us

profile of v2, /device:TPU:0, one launch (start us, length us, event | category | flops | bytes accessed | tf_op | source)
XLA Modules:
  0.0 123.8 jit_solution(989171536968865195)
XLA Ops:
  1.3 119.3 %shard_map.85 = (bf16[128,2048]{1,0:T(8,128)(2,1)S(1)}, bf16[2048,896]{1,0:T(8,128)(2,1)S(1)}, f32[8,128]{1,0:T(8,128)S(1)}) custom-call(s32[4]{0:T(128)} %map_ref.1, s32[5]{0:T(128)} %bounds_ref.1, s32[1]{0:T(128)S(6)} %copy.13.counts_ref, bf16[128,2048]{1,0:T(8,128)(2,1)} %bitcast.8, bf16[4,128,7168]{2,1,0:T(8,128)(2,1)} %t_hbm.1, bf16[2048,896]{1,0:T(8,128)(2,1)} %bitcast.7), custom_call_target="tpu_custom_call" | custom-call | tf_op jit(solution)/shard_map/pallas_call | solution.py:387
  120.6 0.5 slice.3
  121.1 0.8 copy.11
  121.9 1.8 %copy.12 = bf16[1,2048,896]{2,1,0:T(8,128)(2,1)} copy(bf16[1,2048,896]{2,1,0:T(8,128)(2,1)S(1)} %bitcast.5) | data formatting | bytes 7340032

commit v3 on v2

--- a/solution.py
+++ b/solution.py
@@ -63,6 +63,30 @@
 
 def taken_from(here):
     return 1 + 2 * here - 5 * (here // 2)
+
+
+def arrival_order(place, lines):
+    order = []
+    for step in range(lines - 1):
+        sides = (place - 1 - step, place + 1 + step)
+        order += [b for b in (sides if 2 * place < lines else sides[::-1]) if 0 <= b < lines]
+    return order
+
+
+def ring_start(n, steps_a, steps_b):
+    lines = n // 2
+    ring = [2 * p for p in range(lines)] + [2 * (n - 1 - p) + 1 for p in range(lines, n)]
+    for step in range(1, lines - 1):
+        ready = True
+        for place in range(n):
+            line, pair = ring[place] // 2, ring[place] % 2
+            late = [b for k, b in enumerate(arrival_order(line, lines)) if k == 0 or k > step]
+            late = [2 * b + 1 - pair for b in late]
+            needed = [ring[(place + sign * offset) % n] for sign in (1, -1) for offset in (steps_a, -steps_b)]
+            ready = ready and not set(late) & set(needed)
+        if ready:
+            return step
+    return lines - 1
 
 
 def main_kernel(n, direct, map_ref, bounds_ref, counts_ref, s_hbm, t_hbm, w_hbm, sg_ref, pg, loss_ref,
@@ -125,10 +149,7 @@
     def arrival_of(k):
         value = 0
         for place in range(lines):
-            order = []
-            for step in range(lines - 1):
-                order += [b for b in (place - 1 - step, place + 1 + step) if 0 <= b < lines]
-            value = value + order[k] * (reached(place) - reached(place + 1))
+            value = value + arrival_order(place, lines)[k] * (reached(place) - reached(place + 1))
         return value
 
     def piece_of(index, chunk):
@@ -175,10 +196,19 @@
             go_if(from_below & can_up, ag_copy(UP, below, step + 1, chunk))
             pl.when(from_above)(ag_arrival(above, chunk).wait_recv)
             go_if(from_above & can_down, ag_copy(DOWN, above, step + 1, chunk))
+
+    def relay_across(k):
         for chunk in range(CHUNKS):
-            go_if(from_below, ag_copy(ACROSS, below, 2 * step + 1, chunk))
-        for chunk in range(CHUNKS):
-            go_if(from_above, ag_copy(ACROSS, above, 2 * step + 2, chunk))
+            go(ag_copy(ACROSS, 2 * arrival_of(k) + pair, k + 1, chunk))
+
+    def other_line(m):
+        value, bit = 0, 1
+        while bit < lines:
+            mine = (line // bit) % 2
+            flip = (m // bit) % 2
+            value = value + bit * (mine + flip - 2 * mine * flip)
+            bit *= 2
+        return value
 
     def small(source, slots, send_sems, recv_sems, k):
         peer = (me + k) % n
@@ -217,17 +247,17 @@
             device_id=(taker, g), device_id_type=MESH)
 
     def crossing(k):
-        g = 2 * ((line + k) % lines) + 1 - pair
+        g = 2 * other_line(k) + 1 - pair
         return pltpu.make_async_remote_copy(
             src_ref=normed.at[g], dst_ref=passing.at[k], send_sem=p_send.at[k], recv_sem=p_recv.at[k],
             device_id=(here, partner), device_id_type=MESH)
 
     def own_target(k):
-        g = 2 * ((line + k) % lines) + pair
+        g = 2 * other_line(k) + pair
         return target_copy(normed.at[g], me, g)
 
     def passed_target(k):
-        g = 2 * ((line + k) % lines) + pair
+        g = 2 * other_line(k) + pair
         return target_copy(passing.at[k], partner, g)
 
     def target_arrival(index):
@@ -237,7 +267,8 @@
 
     if not direct:
         tgt[block(me), :] = normed[me]
-    for k in range(1, lines):
+    far_first = range(lines - 1, 0, -1)
+    for k in far_first:
         go(crossing(k))
     go(target_copy(normed.at[partner], me, partner))
     if direct:
@@ -312,27 +343,34 @@
 
     load_weights.wait()
     project(me)
+    middle = min(1, lines - 2)
     for step in range(lines - 1):
         relay(step)
-        if step == min(1, lines - 2):
-            for k in range(lines - 1, 0, -1):
+        if step == middle:
+            for k in far_first:
                 go(own_target(k))
+        if step > 0:
+            relay_across(step)
+        if step == lines - 2:
+            relay_across(0)
         project(2 * arrival_of(step) + pair)
         if step == 0:
             for k in range(1, n):
                 small_arrival(counts, c_send, c_recv, k).wait_recv()
             project_across(line)
-        if step == min(1, lines - 2):
-            for k in range(1, lines):
+        if step == middle:
+            for k in far_first:
                 crossing(k).wait_recv()
                 go(passed_target(k))
-    for step in range(lines - 1):
-        project_across(arrival_of(step))
-
-    prepare(0, 1)
-    advance(0, (1,))
-    prepare(0, 0)
-    advance(0, (0,))
+    start = ring_start(n, steps_a, steps_b)
+    for step in range(1, lines):
+        project_across(arrival_of(step % (lines - 1)))
+        if step == start:
+            prepare(0, 0)
+            advance(0, (0,))
+            prepare(0, 1)
+            advance(0, (1,))
+
     for step in range(1, steps_a):
         prepare(step, 1)
         prepare(step, 0)

time: 124 us -> 120 us (0.968)
  Pallas kernels: 119 us -> 116 us
    pallas_call x1, Pallas kernels: 119 us -> 116 us  [per_device(): pl.pallas_call(functools.partial(main_kernel, n, direct), out_shape=(pltp...]
where the time goes in v3:
time: 120 us
  Pallas kernels  116 us (97%)
  local copies, waits for them, and re-layouts  3.14 us (3%)
  between operations  1.29 us (1%)
    pallas_call x1, Pallas kernels, per_device(): pl.pallas_call(functools.partial(main_kernel, n, direct), out_shape=(pltp...  116 us
    unnamed x2, local copies, waits for them, and re-layouts  2.63 us

profile of v3, /device:TPU:0, one launch (start us, length us, event | category | flops | bytes accessed | tf_op | source)
XLA Modules:
  0.0 120.1 jit_solution(6725720781275444887)
XLA Ops:
  1.3 115.7 %shard_map.85 = (bf16[128,2048]{1,0:T(8,128)(2,1)S(1)}, bf16[2048,896]{1,0:T(8,128)(2,1)S(1)}, f32[8,128]{1,0:T(8,128)S(1)}) custom-call(s32[4]{0:T(128)} %map_ref.1, s32[5]{0:T(128)} %bounds_ref.1, s32[1]{0:T(128)S(6)} %copy.13.counts_ref, bf16[128,2048]{1,0:T(8,128)(2,1)} %bitcast.8, bf16[4,128,7168]{2,1,0:T(8,128)(2,1)} %t_hbm.1, bf16[2048,896]{1,0:T(8,128)(2,1)} %bitcast.7), custom_call_target="tpu_custom_call" | custom-call | tf_op jit(solution)/shard_map/pallas_call | solution.py:425
  117.0 0.5 slice.3
  117.5 0.8 copy.11
  118.3 1.8 %copy.12 = bf16[1,2048,896]{2,1,0:T(8,128)(2,1)} copy(bf16[1,2048,896]{2,1,0:T(8,128)(2,1)S(1)} %bitcast.5) | data formatting | bytes 7340032

commit v4 on v3

--- a/solution.py
+++ b/solution.py
@@ -93,7 +93,7 @@
                 teacher, count_ref, weights, stud, normed, tgt, proj, scaled, own, part_a, part_b, got_a, got_b,
                 counts, losses, loss_out,
                 in_sem, slab_sem, w_sem, ag_send, ag_recv, t_send, t_recv, rs_send, rs_recv,
-                c_send, c_recv, l_send, l_recv, passing, p_send, p_recv):
+                c_send, c_recv, l_send, l_recv, passing, p_send, p_recv, rounds):
     here = lax.axis_index("section")
     me = lax.axis_index("dp")
     rows, ds_width = s_hbm.shape
@@ -102,6 +102,10 @@
     steps_a, steps_b = n // 2, n - 1 - n // 2
     teacher_width = width * n
 
+    pair, line = me % 2, me // 2
+    partner = me + 1 - 2 * pair
+    lines = n // 2
+    can_up, can_down = line < lines - 1, line > 0
     x, z = me % 2, me // 2
     position = z * (1 - x) + (n - 1 - z) * x
     sign = 1 - 2 * (here % 2)
@@ -123,25 +127,34 @@
         pltpu.make_async_copy(t_hbm.at[slot], teacher.at[slot], slab_sem.at[slot]) for slot in range(held)
     ]
     barrier = pltpu.get_barrier_semaphore()
-    for k in range(1, n):
-        pl.semaphore_signal(barrier, inc=1, device_id=(here, (me + k) % n), device_id_type=MESH)
-    expected = n - 1
-    if direct:
-        for k in range(n):
-            pl.semaphore_signal(barrier, inc=1, device_id=(send_to(here), (me + k) % n), device_id_type=MESH)
-            pl.semaphore_signal(barrier, inc=1, device_id=(taken_from(here), (me + k) % n), device_id_type=MESH)
-        expected += 2 * n
+    near = 2 - line // (lines - 1) + (line + lines - 1) // lines + 2 * direct
+
+    def greet(semaphore):
+        def signal(section, device):
+            pl.semaphore_signal(semaphore, inc=1, device_id=(section, device), device_id_type=MESH)
+
+        signal(here, partner)
+        pl.when(can_up)(lambda: signal(here, me + 2))
+        pl.when(can_down)(lambda: signal(here, me - 2))
+        if direct:
+            signal(send_to(here), me)
+            signal(taken_from(here), me)
+
+    def next_round(k):
+        if k > 0:
+            pl.semaphore_wait(rounds.at[k - 1], near)
+        if k < lines - 1:
+            greet(rounds.at[k])
+
     load_weights = pltpu.make_async_copy(w_hbm, weights, w_sem)
+    greet(barrier)
     for copy in load_teacher:
         copy.start()
     load_weights.start()
     count_ref[...] = jnp.full(count_ref.shape, counts_ref[0].astype(F32), F32)
-    pl.semaphore_wait(barrier, expected)
+    pl.semaphore_wait(barrier, near)
     load_students.wait()
 
-    pair, line = me % 2, me // 2
-    partner = me + 1 - 2 * pair
-    lines = n // 2
 
     def reached(place):
         return (line + lines - place) // lines
@@ -182,7 +195,6 @@
         pl.when(condition)(copy.start)
         sent_if.append((condition, copy))
 
-    can_up, can_down = line < lines - 1, line > 0
     for chunk in range(CHUNKS):
         go_if(can_up, ag_copy(UP, me, 0, chunk))
         go_if(can_down, ag_copy(DOWN, me, 0, chunk))
@@ -222,9 +234,8 @@
             src_ref=slots.at[peer], dst_ref=slots.at[peer], send_sem=send_sems.at[k],
             recv_sem=recv_sems.at[peer], device_id=(here, peer), device_id_type=MESH)
 
-    for k in range(1, n):
-        go(small(count_ref, counts, c_send, c_recv, k))
     counts[me] = count_ref[...]
+    next_round(0)
 
     for copy in load_teacher:
         copy.wait()
@@ -235,6 +246,7 @@
     for g in range(n):
         h = teacher[place, :, g * width:(g + 1) * width].astype(F32)
         squares += jnp.sum(h * h, axis=1, keepdims=True)
+    next_round(1)
     inverse = lax.rsqrt(squares / teacher_width + norm_eps)
     for g in range(n):
         h = teacher[place, :, g * width:(g + 1) * width].astype(F32)
@@ -270,6 +282,8 @@
     far_first = range(lines - 1, 0, -1)
     for k in far_first:
         go(crossing(k))
+    for k in range(2, lines):
+        next_round(k)
     go(target_copy(normed.at[partner], me, partner))
     if direct:
         go(own_target(0))
@@ -346,6 +360,9 @@
     middle = min(1, lines - 2)
     for step in range(lines - 1):
         relay(step)
+        if step == 0:
+            for k in range(1, n):
+                go(small(count_ref, counts, c_send, c_recv, k))
         if step == middle:
             for k in far_first:
                 go(own_target(k))
@@ -355,14 +372,14 @@
             relay_across(0)
         project(2 * arrival_of(step) + pair)
         if step == 0:
-            for k in range(1, n):
-                small_arrival(counts, c_send, c_recv, k).wait_recv()
             project_across(line)
         if step == middle:
             for k in far_first:
                 crossing(k).wait_recv()
                 go(passed_target(k))
     start = ring_start(n, steps_a, steps_b)
+    for k in range(1, n):
+        small_arrival(counts, c_send, c_recv, k).wait_recv()
     for step in range(1, lines):
         project_across(arrival_of(step % (lines - 1)))
         if step == start:
@@ -464,6 +481,7 @@
             pltpu.VMEM((n // 2, rows, width), BF16),
             dma((n // 2,)),
             dma((n // 2,)),
+            pltpu.SemaphoreType.REGULAR((n // 2 - 1,)),
         ],
         compiler_params=pltpu.CompilerParams(
             collective_id=0, has_side_effects=True, vmem_limit_bytes=56 * 1024 * 1024

time: 120 us -> 119 us (level)
  no operation moved by 1% of the time
where the time goes in v4:
time: 119 us
  Pallas kernels  115 us (97%)
  local copies, waits for them, and re-layouts  3.14 us (3%)
  between operations  1.29 us (1%)
    pallas_call x1, Pallas kernels, per_device(): pl.pallas_call(functools.partial(main_kernel, n, direct), out_shape=(pltp...  115 us
    unnamed x2, local copies, waits for them, and re-layouts  2.63 us

profile of v4, /device:TPU:0, one launch (start us, length us, event | category | flops | bytes accessed | tf_op | source)
XLA Modules:
  0.0 119.1 jit_solution(17359094688123290110)
XLA Ops:
  1.3 114.7 %shard_map.85 = (bf16[128,2048]{1,0:T(8,128)(2,1)S(1)}, bf16[2048,896]{1,0:T(8,128)(2,1)S(1)}, f32[8,128]{1,0:T(8,128)S(1)}) custom-call(s32[4]{0:T(128)} %map_ref.1, s32[5]{0:T(128)} %bounds_ref.1, s32[1]{0:T(128)S(6)} %copy.13.counts_ref, bf16[128,2048]{1,0:T(8,128)(2,1)} %bitcast.8, bf16[4,128,7168]{2,1,0:T(8,128)(2,1)} %t_hbm.1, bf16[2048,896]{1,0:T(8,128)(2,1)} %bitcast.7), custom_call_target="tpu_custom_call" | custom-call | tf_op jit(solution)/shard_map/pallas_call | solution.py:442
  116.0 0.5 slice.3
  116.5 0.8 copy.11
  117.3 1.8 %copy.12 = bf16[1,2048,896]{2,1,0:T(8,128)(2,1)} copy(bf16[1,2048,896]{2,1,0:T(8,128)(2,1)S(1)} %bitcast.5) | data formatting | bytes 7340032

commit v5 on v4

--- a/solution.py
+++ b/solution.py
@@ -426,6 +426,37 @@
         copy.wait_send()
     for condition, copy in sent_if:
         pl.when(condition)(copy.wait_send)
+
+
+def finish_kernel(sg_ref, pg_ref, loss_ref, sg_hbm, pg_hbm, loss_out, sg_sem, pg_sem):
+    size = pg_ref.shape[0] // GRAD_TILES
+    copies = [pltpu.make_async_copy(sg_ref, sg_hbm, sg_sem)]
+    for tile in range(GRAD_TILES):
+        piece = pl.ds(tile * size, size)
+        copies.append(pltpu.make_async_copy(pg_ref.at[piece], pg_hbm.at[piece], pg_sem.at[tile]))
+    for copy in copies:
+        copy.start()
+    loss_out[0] = loss_ref[0, 0]
+    for copy in copies:
+        copy.wait()
+
+
+def finish(student_grad, projector_grad, loss):
+    vmem = pl.BlockSpec(memory_space=pltpu.VMEM)
+    anywhere = pl.BlockSpec(memory_space=pl.ANY)
+    kept = [pltpu.with_memory_space_constraint(x, pltpu.VMEM) for x in (student_grad, projector_grad, loss)]
+    return pl.pallas_call(
+        finish_kernel,
+        out_shape=(
+            jax.ShapeDtypeStruct(student_grad.shape, BF16),
+            jax.ShapeDtypeStruct(projector_grad.shape, BF16),
+            jax.ShapeDtypeStruct((1,), F32),
+        ),
+        in_specs=[vmem, vmem, vmem],
+        out_specs=(anywhere, anywhere, pl.BlockSpec(memory_space=pltpu.SMEM)),
+        scratch_shapes=[pltpu.SemaphoreType.DMA, pltpu.SemaphoreType.DMA((GRAD_TILES,))],
+        compiler_params=pltpu.CompilerParams(vmem_limit_bytes=8 * 1024 * 1024),
+    )(*kept)
 
 
 def per_device(student_states, teacher_states, projector, layer_map, boundaries, valid_counts):
@@ -487,7 +518,8 @@
             collective_id=0, has_side_effects=True, vmem_limit_bytes=56 * 1024 * 1024
         ),
     )(layer_map, boundaries, valid_counts, student_states[0], teacher, projector[0])
-    return student_grad[None], projector_grad[None], loss[0, 0:1]
+    student_grad, projector_grad, loss = finish(student_grad, projector_grad, loss)
+    return student_grad[None], projector_grad[None], loss
 
 
 def solution(mesh):

time: 119 us -> 119 us (level)
  local copies, waits for them, and re-layouts: 3.14 us -> 0 us
  Pallas kernels: 115 us -> 117 us
    unnamed x2 -> x0, local copies, waits for them, and re-layouts: 2.63 us -> none
    pallas_call x0 -> x1, Pallas kernels: none -> 2.59 us  [finish(): pl.pallas_call(finish_kernel, out_shape=(jax.ShapeDtypeStruct(student_gra...]
where the time goes in v5:
time: 119 us
  Pallas kernels  117 us (98%)
  between operations  1.45 us (1%)
    pallas_call x1, Pallas kernels, per_device(): pl.pallas_call(functools.partial(main_kernel, n, direct), out_shape=(pltp...  115 us
    pallas_call x1, Pallas kernels, finish(): pl.pallas_call(finish_kernel, out_shape=(jax.ShapeDtypeStruct(student_gra...  2.59 us

profile of v5, /device:TPU:0, one launch (start us, length us, event | category | flops | bytes accessed | tf_op | source)
XLA Modules:
  0.0 118.7 jit_solution(12971396783327232641)
XLA Ops:
  1.3 114.7 %shard_map.85 = (bf16[128,2048]{1,0:T(8,128)(2,1)S(1)}, bf16[2048,896]{1,0:T(8,128)(2,1)S(1)}, f32[8,128]{1,0:T(8,128)S(1)}) custom-call(s32[4]{0:T(128)} %map_ref.1, s32[5]{0:T(128)} %bounds_ref.1, s32[1]{0:T(128)S(6)} %copy.9.counts_ref, bf16[128,2048]{1,0:T(8,128)(2,1)} %bitcast.5, bf16[4,128,7168]{2,1,0:T(8,128)(2,1)} %t_hbm.1, bf16[2048,896]{1,0:T(8,128)(2,1)} %bitcast.4), custom_call_target="tpu_custom_call" | custom-call | tf_op jit(solution)/shard_map/pallas_call | solution.py:473
  116.0 2.6 %shard_map.86 = (bf16[128,2048]{1,0:T(8,128)(2,1)}, bf16[2048,896]{1,0:T(8,128)(2,1)}, f32[1]{0:T(128)}) custom-call(bf16[128,2048]{1,0:T(8,128)(2,1)S(1)} %get-tuple-element.9.sg_ref, bf16[2048,896]{1,0:T(8,128)(2,1)S(1)} %get-tuple-element.10.pg_ref, f32[8,128]{1,0:T(8,128)S(1)} %get-tuple-element.11.loss_ref), custom_call_target="tpu_custom_call" | custom-call | tf_op jit(solution)/shard_map/pallas_call | solution.py:448

commit v6 on v5

--- a/solution.py
+++ b/solution.py
@@ -11,7 +11,7 @@
 norm_eps = 1e-06
 MESH = pl.DeviceIdType.MESH
 F32, BF16 = jnp.float32, jnp.bfloat16
-CHUNKS = 2
+CHUNKS = 4
 GRAD_TILES = 8
 
 

time: 119 us -> 118 us (level)
  no operation moved by 1% of the time
where the time goes in v6:
time: 118 us
  Pallas kernels  117 us (99%)
  between operations  1.45 us (1%)
    pallas_call x1, Pallas kernels, per_device(): pl.pallas_call(functools.partial(main_kernel, n, direct), out_shape=(pltp...  114 us
    pallas_call x1, Pallas kernels, finish(): pl.pallas_call(finish_kernel, out_shape=(jax.ShapeDtypeStruct(student_gra...  2.59 us

profile of v6, /device:TPU:0, one launch (start us, length us, event | category | flops | bytes accessed | tf_op | source)
XLA Modules:
  0.0 118.1 jit_solution(4688476954134576404)
XLA Ops:
  1.3 114.0 %shard_map.85 = (bf16[128,2048]{1,0:T(8,128)(2,1)S(1)}, bf16[2048,896]{1,0:T(8,128)(2,1)S(1)}, f32[8,128]{1,0:T(8,128)S(1)}) custom-call(s32[4]{0:T(128)} %map_ref.1, s32[5]{0:T(128)} %bounds_ref.1, s32[1]{0:T(128)S(6)} %copy.9.counts_ref, bf16[128,2048]{1,0:T(8,128)(2,1)} %bitcast.5, bf16[4,128,7168]{2,1,0:T(8,128)(2,1)} %t_hbm.1, bf16[2048,896]{1,0:T(8,128)(2,1)} %bitcast.4), custom_call_target="tpu_custom_call" | custom-call | tf_op jit(solution)/shard_map/pallas_call | solution.py:473
  115.3 2.6 %shard_map.86 = (bf16[128,2048]{1,0:T(8,128)(2,1)}, bf16[2048,896]{1,0:T(8,128)(2,1)}, f32[1]{0:T(128)}) custom-call(bf16[128,2048]{1,0:T(8,128)(2,1)S(1)} %get-tuple-element.9.sg_ref, bf16[2048,896]{1,0:T(8,128)(2,1)S(1)} %get-tuple-element.10.pg_ref, f32[8,128]{1,0:T(8,128)S(1)} %get-tuple-element.11.loss_ref), custom_call_target="tpu_custom_call" | custom-call | tf_op jit(solution)/shard_map/pallas_call | solution.py:448
